TPU v7x, 512 devices: a 4x2x32 block of a 4x8x32 slice. The times are simulated.
512 devices in a mesh: groups: 2 (over y), fsdp: 32 (over z), tensor: 8 (over x, core).
Axes of the slice: x: 4, y: 2, z: 32, core: 2. Of those that a mesh axis runs over, the one named last changes fastest.
The devices are a block of a 4x8x32 slice.
Arguments:
- tokens: bfloat16 [16384, 4608], P(('groups', 'fsdp'), 'tensor'), parts along dimension 0, may hold values from -100 to 100
- norm_gain: bfloat16 [4608], P('tensor'), may hold values from 0.25 to 1.75
- w_query: bfloat16 [4608, 4096], P('fsdp', 'tensor'), may hold values from -0.5 to 0.5
- w_key: bfloat16 [4608, 2048], P('fsdp', 'tensor'), may hold values from -0.09375 to 0.09375
- w_value: bfloat16 [4608, 2048], P('fsdp', 'tensor'), may hold values from -0.09375 to 0.09375
- w_out: bfloat16 [4096, 4608], P('tensor', 'fsdp'), may hold values from -0.5 to 0.5
- post_gain: bfloat16 [4608], P('tensor'), may hold values from 0.25 to 1.75
Outputs:
- mixed: float32 [16384, 4608], P(('groups', 'fsdp'), 'tensor'), parts along dimension 0
There are 2 independent parts, one for each index of `groups`. A program takes and returns all parts, laid end to end along the dimension named above; an argument that names none is the same for every part. Nothing has to cross between parts.
All inputs are finite; a program needn't handle non-finite values.
Results may differ from a plain program's by a relative error of at most 0.0053.
Values may be sent and summed in bfloat16 or wider, within the bound.
A program may use at most 128 MiB of HBM per device.

v0:
```python
import jax
import jax.numpy as jnp
from jax import lax
from jax.sharding import PartitionSpec as P

D = 4608
HEAD_DIM = 128
eps_norm = 1e-06
soft_cap = 50.0
attn_scale = 144.0 ** (-0.5)
rope_base = 10000.0


def copy_for_each(array, axis):
    count = lax.axis_size(axis)
    return lax.all_to_all(
        jnp.broadcast_to(array[None], (count, *array.shape)), axis, 0, 0, tiled=True
    )


def of_everyone(array, axis):
    return copy_for_each(array, axis).sum(axis=0)


def joined_along(pieces, dim):
    pieces = jnp.moveaxis(pieces, 0, dim)
    lengths = pieces.shape
    return pieces.reshape(*lengths[:dim], lengths[dim] * lengths[dim + 1], *lengths[dim + 2 :])


def gather_directly(array, axis, dim):
    return joined_along(copy_for_each(array, axis), dim)


def side_by_side(arrays, axis, dim, along):
    ends, at = ([], 0)
    for a in arrays[:-1]:
        at += a.shape[along]
        ends.append(at)
    both = jnp.concatenate(arrays, axis=along)
    return tuple(jnp.split(lax.all_gather(both, axis, axis=dim, tiled=True), ends, axis=along))


def in_blocks(array, dim, count):
    before, after = (array.shape[:dim], array.shape[dim + 1 :])
    return jnp.moveaxis(array.reshape(*before, count, -1, *after), dim, 0)


def summed_on_arrival(array, axis, dim):
    count = lax.axis_size(axis)
    pieces = lax.all_to_all(in_blocks(array, dim, count), axis, 0, 0, tiled=True)
    return jnp.sum(pieces.astype(jnp.float32), axis=0)


def rotate(values, position):
    head_dim = values.shape[-1]
    half = head_dim // 2
    freq = rope_base ** (-(jnp.arange(half, dtype=jnp.float32) * 2.0 / head_dim))
    angle = position.astype(jnp.float32)[:, None] * freq[None, :]
    cosine = jnp.cos(angle)[:, None, :]
    sine = jnp.sin(angle)[:, None, :]
    first = values[..., :half]
    second = values[..., half:]
    return jnp.concatenate(
        [first * cosine - second * sine, second * cosine + first * sine], axis=-1
    )


def attend(query, keys, values, position):
    count, heads, head_dim = query.shape
    kv_count = keys.shape[1]
    grouped = query.reshape(count, kv_count, heads // kv_count, head_dim)
    scores = (
        jnp.einsum("nkgd,mkd->kgnm", grouped, keys, preferred_element_type=jnp.float32) * attn_scale
    )
    capped = soft_cap * jnp.tanh(scores / soft_cap)
    allowed = position[None, :] <= position[:, None]
    weights = jnp.where(allowed, jnp.exp(capped), 0.0)
    probs = (weights / jnp.sum(weights, axis=-1, keepdims=True)).astype(jnp.bfloat16)
    mixed = jnp.einsum("kgnm,mkd->nkgd", probs, values, preferred_element_type=jnp.float32)
    return mixed.reshape(count, heads * head_dim).astype(jnp.bfloat16)


def on_device(tokens, norm_gain, w_query, w_key, w_value, w_out, post_gain):
    rows = tokens.shape[0]
    local = tokens.astype(jnp.float32)
    total = of_everyone(jnp.sum(local * local, axis=1), "tensor")
    normed = (
        local * lax.rsqrt(total / D + eps_norm)[:, None] * norm_gain.astype(jnp.float32)
    ).astype(jnp.bfloat16)
    whole = gather_directly(normed, "tensor", 1)
    pieces = side_by_side((w_query, w_key, w_value), "fsdp", 0, 1)
    query_raw, key_raw, value_raw = tuple(
        (jnp.dot(whole, piece, preferred_element_type=jnp.float32) for piece in pieces)
    )
    position = jnp.arange(rows, dtype=jnp.int32)
    local_heads = w_query.shape[1] // HEAD_DIM
    local_kv = w_key.shape[1] // HEAD_DIM
    query = rotate(query_raw.reshape(rows, local_heads, HEAD_DIM), position).astype(jnp.bfloat16)
    key = rotate(key_raw.reshape(rows, local_kv, HEAD_DIM), position).astype(jnp.bfloat16)
    value = value_raw.astype(jnp.bfloat16).reshape(rows, local_kv, HEAD_DIM)
    attn = attend(query, key, value, position)
    partial_value = jnp.dot(
        attn, lax.all_gather(w_out, "fsdp", axis=1, tiled=True), preferred_element_type=jnp.float32
    )
    proj = summed_on_arrival(partial_value.astype(jnp.bfloat16), "tensor", 1)
    post_total = of_everyone(jnp.sum(proj * proj, axis=1), "tensor")
    branch = proj * lax.rsqrt(post_total / D + eps_norm)[:, None] * post_gain.astype(jnp.float32)
    return tokens.astype(jnp.float32) + branch


def solution(mesh):
    placed = (
        P(("groups", "fsdp"), "tensor"),
        P("tensor"),
        P("fsdp", "tensor"),
        P("fsdp", "tensor"),
        P("fsdp", "tensor"),
        P("tensor", "fsdp"),
        P("tensor"),
    )
    return jax.shard_map(
        on_device,
        mesh=mesh,
        in_specs=placed,
        out_specs=P(("groups", "fsdp"), "tensor"),
        check_vma=False,
    )
```

profile of v0, /device:TPU:33, one launch (start us, length us, event | category | flops | bytes accessed | tf_op | source)
XLA Modules:
  0.0 380.2 jit_solution(6759158152972305025)
XLA Ops:
  6.5 0.0 all-gather.3.cloned.1.call-start
  6.6 1.7 pad_maximum_fusion
  8.3 0.1 all-gather.3.cloned.1.call-update
  8.3 0.1 all-gather.5.cloned.1.call-start
  8.4 0.7 all-gather.5.cloned.1.call-update
  9.2 1.1 fusion.10
  10.2 0.6 broadcast_in_dim.12
  10.8 44.7 %all-to-all-start = ((f32[8,1,256]{2,1,0:T(1,128)}), f32[8,1,256]{2,1,0:T(1,128)S(1)}, u32[]{:S(2)}, u32[]{:S(2)}) async-start(f32[8,1,256]{2,1,0:T(1,128)} %broadcast_in_dim.12), calls=%async_computation | async-start | bytes 16384 | tf_op jit(solution)/shard_map/all_to_all | solution.py:16
  55.5 0.7 convert_element_type.60
  56.2 4.0 %all-to-all-done = f32[8,1,256]{2,1,0:T(1,128)S(1)} async-done(((f32[8,1,256]{2,1,0:T(1,128)}), f32[8,1,256]{2,1,0:T(1,128)S(1)}, u32[]{:S(2)}, u32[]{:S(2)}) %all-to-all-start) | async-done | bytes 8224 | tf_op jit(solution)/shard_map/all_to_all | solution.py:16
  60.2 1.1 fusion.12
  61.3 1.6 broadcast_in_dim.13
  63.0 4.2 %all-to-all-start.1 = ((bf16[8,256,576]{1,2,0:T(8,128)(2,1)}), bf16[8,256,576]{1,2,0:T(8,128)(2,1)S(1)}, u32[]{:S(2)}, u32[]{:S(2)}) async-start(bf16[8,256,576]{1,2,0:T(8,128)(2,1)} %broadcast_in_dim.13), calls=%async_computation.1 | async-start | bytes 4718592 | tf_op jit(solution)/shard_map/all_to_all | solution.py:16
  67.2 0.3 multiply_cosine_fusion
  67.5 102.3 %all-gather.3.cloned.1.call-done = bf16[4608,1024]{1,0:T(8,128)(2,1)} async-done(((bf16[144,1024]{1,0:T(8,128)(2,1)}), bf16[4608,1024]{1,0:T(8,128)(2,1)}) %all-gather.3.cloned.1.call-update) | async-done | bytes 9437200 | tf_op jit(solution)/shard_map/all_gather | solution.py:41
  169.8 4.8 %slice_bitcast_fusion = bf16[512,4608]{0,1:T(8,128)(2,1)} fusion(bf16[4608,1024]{1,0:T(8,128)(2,1)} %all-gather.3.cloned.1.call-done), kind=kLoop, calls=%fused_computation.1 | loop fusion | bytes 9437184 | tf_op jit(solution)/shard_map/dot_general | solution.py:94
  174.6 6.8 %copy.36 = bf16[512,4608]{1,0:T(8,128)(2,1)} copy(bf16[512,4608]{0,1:T(8,128)(2,1)} %slice_bitcast_fusion) | data formatting | bytes 9437184 | tf_op jit(solution)/shard_map/dot_general | solution.py:94
  181.4 0.0 all-to-all-done.1
  181.4 0.0 copy-start.1
  181.4 4.6 %fusion.22 = f32[256,4,128]{0,2,1:T(8,128)S(1)} fusion(bf16[256,4608,1]{0,1,2:T(8,128)(2,1)S(1)} %bitcast.45, bf16[4,128,4608]{2,1,0:T(8,128)(2,1)} %bitcast.44), kind=kOutput, calls=%fused_computation.44 | convolution fusion | flops 1207959552 | bytes 7602176 | tf_op jit(solution)/shard_map/dot_general | solution.py:94
  186.0 0.0 copy-done.1
  186.0 0.1 subtract_convert_fusion
  186.1 0.2 copy.38
  186.2 0.2 copy.39
  186.4 1.8 slice_bitcast_fusion.1
  188.2 2.6 copy.34
  190.8 3.1 fusion.21
  193.9 0.0 copy-start.2
  194.0 0.6 fusion.6
  194.6 1.1 copy-done.2
  195.6 2.8 fusion.7
  198.4 0.3 convolution_convert_fusion.1
  198.7 103.8 %all-gather.5.cloned.1.call-done = bf16[512,4608]{0,1:T(8,128)(2,1)} async-done(((bf16[512,144]{0,1:T(8,128)(2,1)}), bf16[512,4608]{0,1:T(8,128)(2,1)}) %all-gather.5.cloned.1.call-update) | async-done | bytes 4718608 | tf_op jit(solution)/shard_map/all_gather | solution.py:104
  302.5 3.8 convolution_convert_fusion
  306.3 2.5 copy.42
  308.7 53.6 %all_to_all.22 = bf16[8,256,576]{1,2,0:T(8,128)(2,1)S(1)} all-to-all(bf16[8,256,576]{1,2,0:T(8,128)(2,1)} %bitcast.43), channel_id=1, replica_groups=mesh['groups'=2,'fsdp'=32,'tensor'=8] {'tensor'}, dimensions={0} | all-to-all | bytes 4718592 | tf_op jit(solution)/shard_map/all_to_all | solution.py:51
  362.3 0.0 copy-start.3
  362.3 0.0 copy-start
  362.3 0.3 convert_reduce_fusion
  362.6 0.1 multiply_reduce_fusion
  362.7 0.6 broadcast_in_dim.16
  363.3 4.3 %all-to-all-start.3 = ((f32[8,1,256]{2,1,0:T(1,128)}), f32[8,1,256]{2,1,0:T(1,128)S(1)}, u32[]{:S(2)}, u32[]{:S(2)}) async-start(f32[8,1,256]{2,1,0:T(1,128)} %broadcast_in_dim.16), calls=%async_computation.3 | async-start | bytes 16384 | tf_op jit(solution)/shard_map/all_to_all | solution.py:16
  367.6 0.0 copy-done.3
  367.6 4.7 %all-to-all-done.3 = f32[8,1,256]{2,1,0:T(1,128)S(1)} async-done(((f32[8,1,256]{2,1,0:T(1,128)}), f32[8,1,256]{2,1,0:T(1,128)S(1)}, u32[]{:S(2)}, u32[]{:S(2)}) %all-to-all-start.3) | async-done | bytes 8224 | tf_op jit(solution)/shard_map/all_to_all | solution.py:16
  372.4 0.0 copy-done
  372.4 1.0 convert_add_fusion
  (9 shorter events, 0.2 us)
Async XLA Ops:
  6.5 163.2 %all-gather.3.cloned.1.call-start = ((), (), s32[]{:S(2)}) async-start(), calls=%async_computation.4 | async-start | bytes 9732096 | tf_op jit(solution)/shard_map/all_gather | solution.py:41
  8.3 294.2 %all-gather.5.cloned.1.call-start = ((), (), s32[]{:S(2)}) async-start(), calls=%async_computation.5 | async-start | bytes 4866048 | tf_op jit(solution)/shard_map/all_gather | solution.py:104
  10.8 49.4 %all-to-all-start = ((f32[8,1,256]{2,1,0:T(1,128)}), f32[8,1,256]{2,1,0:T(1,128)S(1)}, u32[]{:S(2)}, u32[]{:S(2)}) async-start(f32[8,1,256]{2,1,0:T(1,128)} %broadcast_in_dim.12), calls=%async_computation | async-start | bytes 16384 | tf_op jit(solution)/shard_map/all_to_all | solution.py:16
  63.0 118.4 %all-to-all-start.1 = ((bf16[8,256,576]{1,2,0:T(8,128)(2,1)}), bf16[8,256,576]{1,2,0:T(8,128)(2,1)S(1)}, u32[]{:S(2)}, u32[]{:S(2)}) async-start(bf16[8,256,576]{1,2,0:T(8,128)(2,1)} %broadcast_in_dim.13), calls=%async_computation.1 | async-start | bytes 4718592 | tf_op jit(solution)/shard_map/all_to_all | solution.py:16
  181.4 4.6 %copy-start.1 = (bf16[8,256,576]{1,2,0:T(8,128)(2,1)}, bf16[8,256,576]{1,2,0:T(8,128)(2,1)S(1)}, u32[]{:S(2)}) copy-start(bf16[8,256,576]{1,2,0:T(8,128)(2,1)S(1)} %all-to-all-done.1) | copy-start | bytes 7077892
  193.9 1.7 copy-start.2
  362.3 5.3 %copy-start.3 = (bf16[576]{0:T(1024)(128)(2,1)S(1)}, bf16[576]{0:T(1024)(128)(2,1)}, u32[]{:S(2)}) copy-start(bf16[576]{0:T(1024)(128)(2,1)} %param.13) | copy-start | bytes 3460
  362.3 10.1 %copy-start = (bf16[256,576]{0,1:T(8,128)(2,1)S(1)}, bf16[256,576]{0,1:T(8,128)(2,1)}, u32[]{:S(2)}) copy-start(bf16[256,576]{0,1:T(8,128)(2,1)} %param.7) | copy-start | bytes 884740
  363.3 9.0 %all-to-all-start.3 = ((f32[8,1,256]{2,1,0:T(1,128)}), f32[8,1,256]{2,1,0:T(1,128)S(1)}, u32[]{:S(2)}, u32[]{:S(2)}) async-start(f32[8,1,256]{2,1,0:T(1,128)} %broadcast_in_dim.16), calls=%async_computation.3 | async-start | bytes 16384 | tf_op jit(solution)/shard_map/all_to_all | solution.py:16
Sparse Core Ops, SparseCore 0:
  9.4 160.3 all-gather.2
  171.9 130.5 all-gather.4
where the time goes:
time: 381 us; the launch traced here: 380 us
  waiting for transfers between devices  216 us (57%)
  blocking collectives  53.6 us (14%)
  starting transfers between devices  53.2 us (14%)
  local copies, waits for them, and re-layouts  22.7 us (6%)
  matrix products  15.1 us (4%)
  between operations  13.6 us (4%)
  other arithmetic  6.51 us (2%)
    all_gather x1, waiting for transfers between devices, on_device(): lax.all_gather(w_out, 'fsdp', axis=1, tiled=True)  104 us
    all_gather x1, waiting for transfers between devices, side_by_side(): lax.all_gather(both, axis, axis=dim, tiled=True)  102 us
    all_to_all x1, blocking collectives, summed_on_arrival(): lax.all_to_all(in_blocks(array, dim, count), axis, 0, 0, tiled=True)  53.6 us
    all_to_all x3, starting transfers between devices, copy_for_each(): lax.all_to_all(jnp.broadcast_to(array[None], (count, *array.shape)), axis...  53.1 us
    dot_general x4, local copies, waits for them, and re-layouts, on_device(): jnp.dot(whole, piece, preferred_element_type=jnp.float32)  16 us
    dot_general x3, matrix products, on_device(): jnp.dot(whole, piece, preferred_element_type=jnp.float32)  10.5 us
    all_to_all x3, waiting for transfers between devices, copy_for_each(): lax.all_to_all(jnp.broadcast_to(array[None], (count, *array.shape)), axis...  8.7 us
  transfers between devices with their start and end apart: 5, of which 4 were waited for; matrix products, arithmetic and copies ran while one was open for 9% of the time, Pallas kernels for 0%

commit v1 on v0

--- a/solution.py
+++ b/solution.py
@@ -9,6 +9,11 @@
 soft_cap = 50.0
 attn_scale = 144.0 ** (-0.5)
 rope_base = 10000.0
+
+
+def gather_from_all(array, axis, dim):
+    copies = jnp.concatenate([array] * lax.axis_size(axis), axis=dim)
+    return lax.all_to_all(copies, axis, dim, dim, tiled=True)
 
 
 def copy_for_each(array, axis):
@@ -101,7 +106,7 @@
     value = value_raw.astype(jnp.bfloat16).reshape(rows, local_kv, HEAD_DIM)
     attn = attend(query, key, value, position)
     partial_value = jnp.dot(
-        attn, lax.all_gather(w_out, "fsdp", axis=1, tiled=True), preferred_element_type=jnp.float32
+        attn, gather_from_all(w_out, "fsdp", 1), preferred_element_type=jnp.float32
     )
     proj = summed_on_arrival(partial_value.astype(jnp.bfloat16), "tensor", 1)
     post_total = of_everyone(jnp.sum(proj * proj, axis=1), "tensor")

time: 381 us -> 727 us (1.91)
  waiting for transfers between devices: 216 us -> 534 us
  local copies, waits for them, and re-layouts: 22.7 us -> 55.8 us
  blocking collectives: 53.6 us -> 42.4 us
  starting transfers between devices: 53.2 us -> 60.8 us
    all_gather x1, waiting for transfers between devices: 102 us -> 512 us  [side_by_side(): lax.all_gather(both, axis, axis=dim, tiled=True)]
    all_gather x1 -> x0, waiting for transfers between devices: 104 us -> none  [on_device(): lax.all_gather(w_out, 'fsdp', axis=1, tiled=True)]
    unnamed x8 -> x47, local copies, waits for them, and re-layouts: 1.07 us -> 33.6 us
    all_to_all x3, waiting for transfers between devices: 8.7 us -> 21.6 us  [copy_for_each(): lax.all_to_all(jnp.broadcast_to(array[None], (count, *array.shape)), axis...]
    all_to_all x1, blocking collectives: 53.6 us -> 42.4 us  [summed_on_arrival(): lax.all_to_all(in_blocks(array, dim, count), axis, 0, 0, tiled=True)]
  transfers between devices with their start and end apart: 5 -> 5, of which waited for: 4 -> 3; matrix products, arithmetic and copies ran while one was open for 9% -> 9% of each run, Pallas kernels for 0% -> 0%
where the time goes in v1:
time: 727 us; the launch traced here: 726 us
  waiting for transfers between devices  534 us (73%)
  starting transfers between devices  60.8 us (8%)
  local copies, waits for them, and re-layouts  55.8 us (8%)
  blocking collectives  42.4 us (6%)
  matrix products  14.4 us (2%)
  between operations  13.6 us (2%)
    all_gather x1, waiting for transfers between devices, side_by_side(): lax.all_gather(both, axis, axis=dim, tiled=True)  512 us
    all_to_all x3, starting transfers between devices, copy_for_each(): lax.all_to_all(jnp.broadcast_to(array[None], (count, *array.shape)), axis...  53.8 us
    all_to_all x1, blocking collectives, summed_on_arrival(): lax.all_to_all(in_blocks(array, dim, count), axis, 0, 0, tiled=True)  42.4 us
    unnamed x47, local copies, waits for them, and re-layouts  33.6 us
    all_to_all x3, waiting for transfers between devices, copy_for_each(): lax.all_to_all(jnp.broadcast_to(array[None], (count, *array.shape)), axis...  21.6 us
    dot_general x4, local copies, waits for them, and re-layouts, on_device(): jnp.dot(whole, piece, preferred_element_type=jnp.float32)  16 us
  transfers between devices with their start and end apart: 5, of which 3 were waited for; matrix products, arithmetic and copies ran while one was open for 9% of the time, Pallas kernels for 0%

profile of v1, /device:TPU:33, one launch (start us, length us, event | category | flops | bytes accessed | tf_op | source)
XLA Modules:
  0.0 726.2 jit_solution(4757934049023381167)
XLA Ops:
  6.5 1.1 fusion.10
  7.6 0.6 broadcast_in_dim.12
  8.2 44.7 %all-to-all-start = ((f32[8,1,256]{2,1,0:T(1,128)}), f32[8,1,256]{2,1,0:T(1,128)S(1)}, u32[]{:S(2)}, u32[]{:S(2)}) async-start(f32[8,1,256]{2,1,0:T(1,128)} %broadcast_in_dim.12), calls=%async_computation | async-start | bytes 16384 | tf_op jit(solution)/shard_map/all_to_all | solution.py:21
  52.9 1.6 constant_dynamic-update-slice_fusion.31
  54.5 1.6 constant_dynamic-update-slice_fusion.30
  56.1 1.6 constant_dynamic-update-slice_fusion.29
  57.6 1.6 constant_dynamic-update-slice_fusion.28
  59.2 1.6 constant_dynamic-update-slice_fusion.27
  60.8 1.6 constant_dynamic-update-slice_fusion.26
  62.4 1.6 constant_dynamic-update-slice_fusion.25
  64.0 1.6 constant_dynamic-update-slice_fusion.24
  65.5 1.6 constant_dynamic-update-slice_fusion.23
  67.1 1.7 constant_dynamic-update-slice_fusion.22
  68.8 1.6 constant_dynamic-update-slice_fusion.21
  70.4 1.6 constant_dynamic-update-slice_fusion.20
  72.0 1.6 constant_dynamic-update-slice_fusion.19
  73.5 1.6 constant_dynamic-update-slice_fusion.18
  75.1 0.7 convert_element_type.60
  75.8 1.1 fusion.12
  77.0 1.6 broadcast_in_dim.13
  78.5 4.9 all-to-all-start.1
  83.4 0.7 constant_dynamic-update-slice_fusion.17
  84.1 0.7 constant_dynamic-update-slice_fusion.16
  84.7 0.7 constant_dynamic-update-slice_fusion.15
  85.4 0.7 constant_dynamic-update-slice_fusion.14
  86.1 0.7 constant_dynamic-update-slice_fusion.13
  86.7 0.7 constant_dynamic-update-slice_fusion.12
  87.4 0.7 constant_dynamic-update-slice_fusion.11
  88.1 0.7 constant_dynamic-update-slice_fusion.10
  88.8 0.7 constant_dynamic-update-slice_fusion.9
  89.4 0.7 constant_dynamic-update-slice_fusion.8
  90.1 0.7 constant_dynamic-update-slice_fusion.7
  90.8 0.7 constant_dynamic-update-slice_fusion.6
  91.4 0.7 constant_dynamic-update-slice_fusion.5
  92.1 0.7 constant_dynamic-update-slice_fusion.4
  92.8 0.7 constant_dynamic-update-slice_fusion.3
  93.5 0.7 constant_dynamic-update-slice_fusion.2
  94.1 0.7 constant_dynamic-update-slice_fusion.1
  94.8 0.7 constant_dynamic-update-slice_fusion
  95.5 16.9 %all-to-all-done.1 = bf16[8,256,576]{1,2,0:T(8,128)(2,1)S(1)} async-done(((bf16[8,256,576]{1,2,0:T(8,128)(2,1)}), bf16[8,256,576]{1,2,0:T(8,128)(2,1)S(1)}, u32[]{:S(2)}, u32[]{:S(2)}) %all-to-all-start.1) | async-done | bytes 2359328 | tf_op jit(solution)/shard_map/all_to_all | solution.py:21
  112.4 6.9 all-to-all-start.2
  119.4 0.7 pad_maximum_fusion
  120.3 0.3 multiply_cosine_fusion
  120.6 511.9 %all-gather.2.cloned.1.call-done = bf16[4608,1024]{1,0:T(8,128)(2,1)} async-done(((bf16[144,1024]{1,0:T(8,128)(2,1)}), bf16[4608,1024]{1,0:T(8,128)(2,1)}) %all-gather.2.cloned.1.call-update) | async-done | bytes 9437200 | tf_op jit(solution)/shard_map/all_gather | solution.py:46
  632.5 4.7 slice_bitcast_fusion
  637.3 6.8 copy.36
  644.1 3.7 fusion.22
  647.9 0.2 copy.38
  648.0 0.2 copy.39
  648.2 1.8 slice_bitcast_fusion.1
  650.1 2.6 copy.34
  652.7 3.3 fusion.21
  656.0 0.6 fusion.6
  656.6 2.8 fusion.7
  659.4 0.3 convolution_convert_fusion.1
  659.7 3.8 convolution_convert_fusion
  663.5 2.5 copy.42
  666.0 42.4 %all_to_all.34 = bf16[8,256,576]{1,2,0:T(8,128)(2,1)S(1)} all-to-all(bf16[8,256,576]{1,2,0:T(8,128)(2,1)} %bitcast.45), channel_id=1, replica_groups=mesh['groups'=2,'fsdp'=32,'tensor'=8] {'tensor'}, dimensions={0} | all-to-all | bytes 4718592 | tf_op jit(solution)/shard_map/all_to_all | solution.py:56
  708.3 0.3 convert_reduce_fusion
  708.7 0.1 multiply_reduce_fusion
  708.8 0.6 broadcast_in_dim.16
  709.4 4.3 all-to-all-start.4
  713.7 4.7 all-to-all-done.4
  718.4 1.0 convert_add_fusion
  (30 shorter events, 0.4 us)
Async XLA Ops:
  8.2 67.6 %all-to-all-start = ((f32[8,1,256]{2,1,0:T(1,128)}), f32[8,1,256]{2,1,0:T(1,128)S(1)}, u32[]{:S(2)}, u32[]{:S(2)}) async-start(f32[8,1,256]{2,1,0:T(1,128)} %broadcast_in_dim.12), calls=%async_computation | async-start | bytes 16384 | tf_op jit(solution)/shard_map/all_to_all | solution.py:21
  67.1 16.3 %copy-start = (bf16[512,144]{0,1:T(8,128)(2,1)S(1)}, bf16[512,144]{0,1:T(8,128)(2,1)}, u32[]{:S(2)}) copy-start(bf16[512,144]{0,1:T(8,128)(2,1)} %param.12) | copy-start | bytes 442372
  78.5 33.9 %all-to-all-start.1 = ((bf16[8,256,576]{1,2,0:T(8,128)(2,1)}), bf16[8,256,576]{1,2,0:T(8,128)(2,1)S(1)}, u32[]{:S(2)}, u32[]{:S(2)}) async-start(bf16[8,256,576]{1,2,0:T(8,128)(2,1)} %broadcast_in_dim.13), calls=%async_computation.1 | async-start | bytes 4718592 | tf_op jit(solution)/shard_map/all_to_all | solution.py:21
  112.4 531.6 %copy-start.2 = (bf16[8,256,576]{1,2,0:T(8,128)(2,1)}, bf16[8,256,576]{1,2,0:T(8,128)(2,1)S(1)}, u32[]{:S(2)}) copy-start(bf16[8,256,576]{1,2,0:T(8,128)(2,1)S(1)} %all-to-all-done.1) | copy-start | bytes 7077892
  112.4 7.0 copy-start.4
  112.4 7.0 copy-start.5
  112.4 7.0 copy-start.6
  112.4 547.3 %all-to-all-start.2 = ((bf16[512,32,144]{0,2,1:T(8,128)(2,1)}), bf16[512,32,144]{0,2,1:T(8,128)(2,1)}, u32[]{:S(2)}, u32[]{:S(2)}) async-start(bf16[512,32,144]{0,2,1:T(8,128)(2,1)} %bitcast.18), calls=%async_computation.2 | async-start | bytes 9437184 | tf_op jit(solution)/shard_map/all_to_all | solution.py:16
  119.3 513.2 %all-gather.2.cloned.1.call-start = ((), (), s32[]{:S(2)}) async-start(), calls=%async_computation.5 | async-start | bytes 9732096 | tf_op jit(solution)/shard_map/all_gather | solution.py:46
  652.7 3.9 copy-start.3
  666.0 47.7 %copy-start.7 = (bf16[576]{0:T(1024)(128)(2,1)S(1)}, bf16[576]{0:T(1024)(128)(2,1)}, u32[]{:S(2)}) copy-start(bf16[576]{0:T(1024)(128)(2,1)} %param.13) | copy-start | bytes 3460
  666.0 52.4 %copy-start.1 = (bf16[256,576]{0,1:T(8,128)(2,1)S(1)}, bf16[256,576]{0,1:T(8,128)(2,1)}, u32[]{:S(2)}) copy-start(bf16[256,576]{0,1:T(8,128)(2,1)} %param.7) | copy-start | bytes 884740
  709.4 9.0 %all-to-all-start.4 = ((f32[8,1,256]{2,1,0:T(1,128)}), f32[8,1,256]{2,1,0:T(1,128)S(1)}, u32[]{:S(2)}, u32[]{:S(2)}) async-start(f32[8,1,256]{2,1,0:T(1,128)} %broadcast_in_dim.16), calls=%async_computation.4 | async-start | bytes 16384 | tf_op jit(solution)/shard_map/all_to_all | solution.py:21
Sparse Core Ops, SparseCore 0:
  122.3 510.2 all-gather.1
